TPU v7x, 128 devices: a whole 4x4x4 slice. The times are simulated.
128 devices in a mesh: row: 8 (over z, core), col: 16 (over y, x).
Axes of the slice: x: 4, y: 4, z: 4, core: 2. Of those that a mesh axis runs over, the one named last changes fastest.
Arguments:
- right_side: float32 [512, 4096], P('row', 'col'), may hold values from -20 to 20
- initial_guess: float32 [512, 4096], P('row', 'col'), may hold values from -3 to 3
- kernel: float32 [31, 31], replicated, may hold values from 0 to 1, as said below
Outputs:
- template: float32 [512, 4096], P('row', 'col')
- residual: float32 [512, 4096], P('row', 'col')
Inputs may be any that keep to these rules, and one draw needn't show every extreme that they name: `kernel`: entries are positive and sum to one.
All inputs are finite; a program needn't handle non-finite values.
Results may differ from a plain program's by a relative error of at most 0.0003.
Values sent between devices are 32-bit elements; how exact they have to be, the bound alone decides.
A program may use at most 128 MiB of HBM per device.

v0:
```python
import math
import jax
import jax.numpy as jnp
from jax import lax
from jax.sharding import Mesh
from jax.sharding import PartitionSpec as P

ITERS = 3
ROW_COL = ("row_0", "row_1", "col_0", "col_1")
ROW = ("row_0", "row_1")
COL = ("col_0", "col_1")
penalty = 0.05


def with_halo(x, sides, width):
    for axis, dim in sides:
        count, length = (lax.axis_size(axis), x.shape[dim])
        up = [(i, (i + 1) % count) for i in range(count - 1)]
        down = [(j, i) for i, j in up]
        last = lax.slice_in_dim(x, length - width, length, axis=dim)
        initial = lax.slice_in_dim(x, 0, width, axis=dim)
        before = lax.ppermute(last, axis, up)
        after = lax.ppermute(initial, axis, down)
        x = jnp.concatenate([before, x, after], axis=dim)
    return x


def one_axis_at_a_time(x, axes):
    for axis in axes:
        x = lax.psum(x, axis)
    return x


def banded_tables(taps, block_width):
    width = taps.shape[0]
    span = block_width + width - 1
    offset = (
        jnp.arange(span, dtype=jnp.int32)[:, None]
        - jnp.arange(block_width, dtype=jnp.int32)[None, :]
    )
    selector = (offset[None, :, :] == jnp.arange(width, dtype=jnp.int32)[:, None, None]).astype(
        jnp.float32
    )
    return jnp.einsum("ab,bkj->akj", taps, selector, precision=lax.Precision.HIGHEST)


def correlate(padded, taps):
    width = taps.shape[0]
    out_rows = padded.shape[0] - width + 1
    out_cols = padded.shape[1] - width + 1
    block_width = math.gcd(out_cols, 128)
    count = out_cols // block_width
    span = block_width + width - 1
    tables = banded_tables(taps, block_width)
    blocks = jnp.stack(
        [padded[:, index * block_width : index * block_width + span] for index in range(count)],
        axis=1,
    )
    total = jnp.zeros((out_rows, count, block_width), jnp.float32)
    for shift_row in range(width):
        window = blocks[shift_row : shift_row + out_rows]
        total = total + jnp.einsum(
            "rnk,kj->rnj", window, tables[shift_row], precision=lax.Precision.HIGHEST
        )
    return total.reshape(out_rows, out_cols)


def laplacian(padded, margin, tile_rows, tile_cols):
    center = padded[margin : margin + tile_rows, margin : margin + tile_cols]
    upper = padded[margin - 1 : margin - 1 + tile_rows, margin : margin + tile_cols]
    lower = padded[margin + 1 : margin + 1 + tile_rows, margin : margin + tile_cols]
    leftward = padded[margin : margin + tile_rows, margin - 1 : margin - 1 + tile_cols]
    rightward = padded[margin : margin + tile_rows, margin + 1 : margin + 1 + tile_cols]
    return 4.0 * center - upper - lower - leftward - rightward


def operate(source, kernel):
    tile_rows, tile_cols = source.shape
    half_width = kernel.shape[0] // 2
    flipped = kernel[::-1, ::-1]
    padded = with_halo(source, ((ROW, 0), (COL, 1)), half_width)
    blurred = correlate(padded, kernel)
    blurred_pad = with_halo(blurred, ((ROW, 0), (COL, 1)), half_width)
    back = correlate(blurred_pad, flipped)
    smooth_term = laplacian(padded, half_width, tile_rows, tile_cols)
    return back + penalty * smooth_term


def paired(residual, applied):
    return (
        one_axis_at_a_time(jnp.sum(residual * residual), ROW_COL),
        one_axis_at_a_time(jnp.sum(residual * applied), ROW_COL),
    )


def on_device(right_side, initial_guess, kernel):
    template = initial_guess
    residual = right_side - operate(template, kernel)
    applied = operate(residual, kernel)
    norm_now, product = paired(residual, applied)
    step_size = norm_now / product
    direction, along = (residual, applied)
    for iteration in range(ITERS):
        template = template + step_size * direction
        residual = residual - step_size * along
        if iteration + 1 < ITERS:
            applied = operate(residual, kernel)
            norm_next, product = paired(residual, applied)
            ratio = norm_next / norm_now
            step_size = norm_next / (product - ratio * norm_next / step_size)
            direction = residual + ratio * direction
            along = applied + ratio * along
            norm_now = norm_next
    return (template, residual)


def solution(mesh):
    torus = Mesh(mesh.devices.reshape(4, 2, 4, 4), ("row_0", "row_1", "col_0", "col_1"))
    placed = (P(ROW, COL), P(ROW, COL), P())
    return jax.shard_map(
        on_device,
        mesh=torus,
        in_specs=placed,
        out_specs=(P(ROW, COL), P(ROW, COL)),
        check_vma=False,
    )
```

profile of v0, /device:TPU:2, one launch (start us, length us, event | category | flops | bytes accessed | tf_op | source)
XLA Modules:
  0.0 353.5 jit_solution(8451478255131608723)
XLA Ops:
  1.4 1.7 collective-permute-start
  5.2 2.0 fusion.2
  7.3 1.3 fusion.3
  8.6 1.3 fusion.1273
  10.0 1.3 fusion.1275
  11.4 1.9 collective-permute-start.3
  13.4 4.1 %collective-permute-start.2 = (f32[94,15]{1,0:T(8,128)S(1)}, f32[94,15]{1,0:T(8,128)S(1)}, u32[]{:S(2)}, u32[]{:S(2)}) collective-permute-start(f32[94,15]{1,0:T(8,128)S(1)} %get-tuple-element.128), channel_id=1, source_target_pairs={{0,1},{1,2},{2,3},{3,4},{4,5},{5,6},{6,7},{7,8},{8,9},{9,10},{10,1... | collective-permute-start | bytes 16928 | tf_op jit(solution)/shard_map/ppermute | solution.py:22
  29.3 4.4 %collective-permute-start.4 = (f32[15,256]{1,0:T(8,128)S(1)}, f32[15,256]{1,0:T(8,128)S(1)}, u32[]{:S(2)}, u32[]{:S(2)}) collective-permute-start(f32[15,256]{1,0:T(8,128)S(1)} %bitcast.674), channel_id=1, source_target_pairs={{0,16},{16,32},{32,48},{48,64},{64,80},{80,96},{96,112},{1,17},{17... | collective-permute-start | bytes 46088 | tf_op jit(solution)/shard_map/ppermute | solution.py:22
  34.7 1.9 collective-permute-start.7
  36.6 4.1 %collective-permute-start.6 = (f32[94,15]{1,0:T(8,128)S(1)}, f32[94,15]{1,0:T(8,128)S(1)}, u32[]{:S(2)}, u32[]{:S(2)}) collective-permute-start(f32[94,15]{1,0:T(8,128)S(1)} %get-tuple-element.124), channel_id=1, source_target_pairs={{0,1},{1,2},{2,3},{3,4},{4,5},{5,6},{6,7},{7,8},{8,9},{9,10},{10,1... | collective-permute-start | bytes 16928 | tf_op jit(solution)/shard_map/ppermute | solution.py:22
  51.3 3.9 %collective-permute-start.8 = (f32[15,256]{1,0:T(8,128)S(1)}, f32[15,256]{1,0:T(8,128)S(1)}, u32[]{:S(2)}, u32[]{:S(2)}) collective-permute-start(f32[15,256]{1,0:T(8,128)S(1)} %get-tuple-element.141), channel_id=1, source_target_pairs={{0,16},{16,32},{32,48},{48,64},{64,80},{80,96},{96,112},{1,17},{17... | collective-permute-start | bytes 46088 | tf_op jit(solution)/shard_map/ppermute | solution.py:22
  56.5 4.7 %collective-permute-done.9 = f32[15,256]{1,0:T(8,128)S(1)} collective-permute-done((f32[15,256]{1,0:T(8,128)S(1)}, f32[15,256]{1,0:T(8,128)S(1)}, u32[]{:S(2)}, u32[]{:S(2)}) %collective-permute-start.9) | collective-permute-done | bytes 15392 | tf_op jit(solution)/shard_map/ppermute | solution.py:23
  61.3 3.9 %collective-permute-start.10 = (f32[94,15]{1,0:T(8,128)S(1)}, f32[94,15]{1,0:T(8,128)S(1)}, u32[]{:S(2)}, u32[]{:S(2)}) collective-permute-start(f32[94,15]{1,0:T(8,128)S(1)} %get-tuple-element.119), channel_id=1, source_target_pairs={{0,1},{1,2},{2,3},{3,4},{4,5},{5,6},{6,7},{7,8},{8,9},{9,10},{10,1... | collective-permute-start | bytes 16928 | tf_op jit(solution)/shard_map/ppermute | solution.py:22
  65.3 2.2 collective-permute-start.11
  67.5 5.8 %collective-permute-done.11 = f32[94,15]{1,0:T(8,128)S(1)} collective-permute-done((f32[94,15]{1,0:T(8,128)S(1)}, f32[94,15]{1,0:T(8,128)S(1)}, u32[]{:S(2)}, u32[]{:S(2)}) %collective-permute-start.11) | collective-permute-done | bytes 5672 | tf_op jit(solution)/shard_map/ppermute | solution.py:23
  83.4 3.8 %collective-permute-start.12 = (f32[15,256]{1,0:T(8,128)S(1)}, f32[15,256]{1,0:T(8,128)S(1)}, u32[]{:S(2)}, u32[]{:S(2)}) collective-permute-start(f32[15,256]{1,0:T(8,128)S(1)} %bitcast.675), channel_id=1, source_target_pairs={{0,16},{16,32},{32,48},{48,64},{64,80},{80,96},{96,112},{1,17},{17... | collective-permute-start | bytes 46088 | tf_op jit(solution)/shard_map/ppermute | solution.py:22
  88.1 1.9 collective-permute-start.15
  90.1 6.7 %collective-permute-start.14 = (f32[94,15]{1,0:T(8,128)S(1)}, f32[94,15]{1,0:T(8,128)S(1)}, u32[]{:S(2)}, u32[]{:S(2)}) collective-permute-start(f32[94,15]{1,0:T(8,128)S(1)} %get-tuple-element.116), channel_id=1, source_target_pairs={{0,1},{1,2},{2,3},{3,4},{4,5},{5,6},{6,7},{7,8},{8,9},{9,10},{10,1... | collective-permute-start | bytes 16928 | tf_op jit(solution)/shard_map/ppermute | solution.py:22
  96.8 1.4 collective-permute-done.14
  107.6 14.4 %all-reduce.8 = (f32[]{:T(128)}, f32[]{:T(128)}) all-reduce(f32[]{:T(128)} %get-tuple-element.7, f32[]{:T(128)} %get-tuple-element.6), channel_id=1, replica_groups=mesh['row_0'=4,'row_1'=2,'col_0'=4,'col_1'=4] {'row_0'}, use_global_device_ids=true, to_apply=%region_1.0 | all-reduce | flops 2 | bytes 16 | tf_op jit(solution)/shard_map/psum | solution.py:30
  122.0 3.1 all-reduce.11
  125.1 16.4 %all-reduce.5 = (f32[]{:T(128)}, f32[]{:T(128)}) all-reduce(f32[]{:T(128)} %get-tuple-element.30, f32[]{:T(128)} %get-tuple-element.31), channel_id=1, replica_groups=mesh['row_0'=4,'row_1'=2,'col_0'=4,'col_1'=4] {'col_0'}, use_global_device_ids=true, to_apply=%region_3.0 | all-reduce | flops 2 | bytes 16 | tf_op jit(solution)/shard_map/psum | solution.py:30
  141.4 12.5 %all-reduce.2 = (f32[]{:T(128)}, f32[]{:T(128)}) all-reduce(f32[]{:T(128)} %get-tuple-element.18, f32[]{:T(128)} %get-tuple-element.19), channel_id=1, replica_groups=mesh['row_0'=4,'row_1'=2,'col_0'=4,'col_1'=4] {'col_1'}, use_global_device_ids=true, to_apply=%region_4.0 | all-reduce | flops 2 | bytes 16 | tf_op jit(solution)/shard_map/psum | solution.py:30
  157.8 1.8 collective-permute-done.17
  159.7 1.9 collective-permute-start.18
  161.6 4.6 %collective-permute-start.19 = (f32[94,15]{1,0:T(8,128)S(1)}, f32[94,15]{1,0:T(8,128)S(1)}, u32[]{:S(2)}, u32[]{:S(2)}) collective-permute-start(f32[94,15]{1,0:T(8,128)S(1)} %get-tuple-element.112), channel_id=1, source_target_pairs={{1,0},{2,1},{3,2},{4,3},{5,4},{6,5},{7,6},{8,7},{9,8},{10,9},{11,1... | collective-permute-start | bytes 16928 | tf_op jit(solution)/shard_map/ppermute | solution.py:23
  166.2 1.5 collective-permute-done.19
  185.8 3.2 collective-permute-start.20
  190.0 3.7 %collective-permute-start.23 = (f32[94,15]{1,0:T(8,128)S(1)}, f32[94,15]{1,0:T(8,128)S(1)}, u32[]{:S(2)}, u32[]{:S(2)}) collective-permute-start(f32[94,15]{1,0:T(8,128)S(1)} %get-tuple-element.107), channel_id=1, source_target_pairs={{1,0},{2,1},{3,2},{4,3},{5,4},{6,5},{7,6},{8,7},{9,8},{10,9},{11,1... | collective-permute-start | bytes 16928 | tf_op jit(solution)/shard_map/ppermute | solution.py:23
  193.7 2.3 collective-permute-start.22
  196.0 3.8 %collective-permute-done.22 = f32[94,15]{1,0:T(8,128)S(1)} collective-permute-done((f32[94,15]{1,0:T(8,128)S(1)}, f32[94,15]{1,0:T(8,128)S(1)}, u32[]{:S(2)}, u32[]{:S(2)}) %collective-permute-start.22) | collective-permute-done | bytes 5672 | tf_op jit(solution)/shard_map/ppermute | solution.py:22
  208.4 1.4 multiply_reduce_fusion.2
  209.8 12.8 %all-reduce.7 = (f32[]{:T(128)}, f32[]{:T(128)}) all-reduce(f32[]{:T(128)} %get-tuple-element.5, f32[]{:T(128)} %get-tuple-element.4), channel_id=1, replica_groups=mesh['row_0'=4,'row_1'=2,'col_0'=4,'col_1'=4] {'row_0'}, use_global_device_ids=true, to_apply=%region_11.0 | all-reduce | flops 2 | bytes 16 | tf_op jit(solution)/shard_map/psum | solution.py:30
  222.5 3.1 all-reduce.10
  225.7 10.3 %all-reduce.4 = (f32[]{:T(128)}, f32[]{:T(128)}) all-reduce(f32[]{:T(128)} %get-tuple-element.28, f32[]{:T(128)} %get-tuple-element.29), channel_id=1, replica_groups=mesh['row_0'=4,'row_1'=2,'col_0'=4,'col_1'=4] {'col_0'}, use_global_device_ids=true, to_apply=%region_13.0 | all-reduce | flops 2 | bytes 16 | tf_op jit(solution)/shard_map/psum | solution.py:30
  236.0 12.5 %all-reduce.1 = (f32[]{:T(128)}, f32[]{:T(128)}) all-reduce(f32[]{:T(128)} %get-tuple-element.16, f32[]{:T(128)} %get-tuple-element.17), channel_id=1, replica_groups=mesh['row_0'=4,'row_1'=2,'col_0'=4,'col_1'=4] {'col_1'}, use_global_device_ids=true, to_apply=%region_14.0 | all-reduce | flops 2 | bytes 16 | tf_op jit(solution)/shard_map/psum | solution.py:30
  256.3 2.4 collective-permute-done.25
  258.8 1.9 collective-permute-start.26
  260.7 4.3 %collective-permute-start.27 = (f32[94,15]{1,0:T(8,128)S(1)}, f32[94,15]{1,0:T(8,128)S(1)}, u32[]{:S(2)}, u32[]{:S(2)}) collective-permute-start(f32[94,15]{1,0:T(8,128)S(1)} %get-tuple-element.104), channel_id=1, source_target_pairs={{1,0},{2,1},{3,2},{4,3},{5,4},{6,5},{7,6},{8,7},{9,8},{10,9},{11,1... | collective-permute-start | bytes 16928 | tf_op jit(solution)/shard_map/ppermute | solution.py:23
  265.0 1.8 collective-permute-done.27
  284.9 3.9 %collective-permute-start.28 = (f32[15,256]{1,0:T(8,128)S(1)}, f32[15,256]{1,0:T(8,128)S(1)}, u32[]{:S(2)}, u32[]{:S(2)}) collective-permute-start(f32[15,256]{1,0:T(8,128)S(1)} %bitcast.673), channel_id=1, source_target_pairs={{0,16},{16,32},{32,48},{48,64},{64,80},{80,96},{96,112},{1,17},{17... | collective-permute-start | bytes 46088 | tf_op jit(solution)/shard_map/ppermute | solution.py:22
  289.7 3.6 %collective-permute-start.31 = (f32[94,15]{1,0:T(8,128)S(1)}, f32[94,15]{1,0:T(8,128)S(1)}, u32[]{:S(2)}, u32[]{:S(2)}) collective-permute-start(f32[94,15]{1,0:T(8,128)S(1)} %get-tuple-element.99), channel_id=1, source_target_pairs={{1,0},{2,1},{3,2},{4,3},{5,4},{6,5},{7,6},{8,7},{9,8},{10,9},{11,1... | collective-permute-start | bytes 16928 | tf_op jit(solution)/shard_map/ppermute | solution.py:23
  293.4 2.5 collective-permute-start.30
  295.9 3.5 collective-permute-done.30
  308.8 13.0 %all-reduce.6 = (f32[]{:T(128)}, f32[]{:T(128)}) all-reduce(f32[]{:T(128)} %get-tuple-element.3, f32[]{:T(128)} %get-tuple-element.2), channel_id=1, replica_groups=mesh['row_0'=4,'row_1'=2,'col_0'=4,'col_1'=4] {'row_0'}, use_global_device_ids=true, to_apply=%region_21.0 | all-reduce | flops 2 | bytes 16 | tf_op jit(solution)/shard_map/psum | solution.py:30
  321.8 3.2 all-reduce.9
  324.9 11.2 %all-reduce.3 = (f32[]{:T(128)}, f32[]{:T(128)}) all-reduce(f32[]{:T(128)} %get-tuple-element.26, f32[]{:T(128)} %get-tuple-element.27), channel_id=1, replica_groups=mesh['row_0'=4,'row_1'=2,'col_0'=4,'col_1'=4] {'col_0'}, use_global_device_ids=true, to_apply=%region_23.0 | all-reduce | flops 2 | bytes 16 | tf_op jit(solution)/shard_map/psum | solution.py:30
  336.1 12.5 %all-reduce = (f32[]{:T(128)}, f32[]{:T(128)}) all-reduce(f32[]{:T(128)} %get-tuple-element.14, f32[]{:T(128)} %get-tuple-element.15), channel_id=1, replica_groups=mesh['row_0'=4,'row_1'=2,'col_0'=4,'col_1'=4] {'col_1'}, use_global_device_ids=true, to_apply=%region_24.0 | all-reduce | flops 2 | bytes 16 | tf_op jit(solution)/shard_map/psum | solution.py:30
  (460 shorter events, 108.2 us)
Async XLA Ops:
  1.4 9.9 %collective-permute-start = (f32[15,256]{1,0:T(8,128)S(1)}, f32[15,256]{1,0:T(8,128)S(1)}, u32[]{:S(2)}, u32[]{:S(2)}) collective-permute-start(f32[15,256]{1,0:T(8,128)S(1)} %get-tuple-element.145), channel_id=1, source_target_pairs={{0,16},{16,32},{32,48},{48,64},{64,80},{80,96},{96,112},{1,17},{17... | collective-permute-start | bytes 46088 | tf_op jit(solution)/shard_map/ppermute | solution.py:22
  3.1 8.2 %collective-permute-start.1 = (f32[15,256]{1,0:T(8,128)S(1)}, f32[15,256]{1,0:T(8,128)S(1)}, u32[]{:S(2)}, u32[]{:S(2)}) collective-permute-start(f32[15,256]{1,0:T(8,128)S(1)} %get-tuple-element.146), channel_id=1, source_target_pairs={{16,0},{32,16},{48,32},{64,48},{80,64},{96,80},{112,96},{17,1},{33... | collective-permute-start | bytes 46088 | tf_op jit(solution)/shard_map/ppermute | solution.py:23
  11.4 6.9 %collective-permute-start.3 = (f32[94,15]{1,0:T(8,128)S(1)}, f32[94,15]{1,0:T(8,128)S(1)}, u32[]{:S(2)}, u32[]{:S(2)}) collective-permute-start(f32[94,15]{1,0:T(8,128)S(1)} %get-tuple-element.127), channel_id=1, source_target_pairs={{1,0},{2,1},{3,2},{4,3},{5,4},{6,5},{7,6},{8,7},{9,8},{10,9},{11,1... | collective-permute-start | bytes 16928 | tf_op jit(solution)/shard_map/ppermute | solution.py:23
  13.4 6.0 %collective-permute-start.2 = (f32[94,15]{1,0:T(8,128)S(1)}, f32[94,15]{1,0:T(8,128)S(1)}, u32[]{:S(2)}, u32[]{:S(2)}) collective-permute-start(f32[94,15]{1,0:T(8,128)S(1)} %get-tuple-element.128), channel_id=1, source_target_pairs={{0,1},{1,2},{2,3},{3,4},{4,5},{5,6},{6,7},{7,8},{8,9},{9,10},{10,1... | collective-permute-start | bytes 16928 | tf_op jit(solution)/shard_map/ppermute | solution.py:22
  18.3 56.9 %copy-start.38 = (f32[1,158,128]{2,0,1:T(1,128)}, f32[1,158,128]{2,0,1:T(1,128)S(1)}, u32[]{:S(2)}) copy-start(f32[1,158,128]{2,0,1:T(1,128)S(1)} %get-tuple-element.90) | copy-start | bytes 242692
  18.3 57.2 %copy-start.37 = (f32[1,158,128]{2,0,1:T(1,128)}, f32[1,158,128]{2,0,1:T(1,128)S(1)}, u32[]{:S(2)}) copy-start(f32[1,158,128]{2,0,1:T(1,128)S(1)} %get-tuple-element.89) | copy-start | bytes 242692
  18.3 57.4 %copy-start.33 = (f32[1,158,128]{2,0,1:T(1,128)}, f32[1,158,128]{2,0,1:T(1,128)S(1)}, u32[]{:S(2)}) copy-start(f32[1,158,128]{2,0,1:T(1,128)S(1)} %get-tuple-element.88) | copy-start | bytes 242692
  18.3 57.7 %copy-start.27 = (f32[1,158,128]{2,0,1:T(1,128)}, f32[1,158,128]{2,0,1:T(1,128)S(1)}, u32[]{:S(2)}) copy-start(f32[1,158,128]{2,0,1:T(1,128)S(1)} %get-tuple-element.87) | copy-start | bytes 242692
  18.3 58.0 %copy-start.21 = (f32[1,158,128]{2,0,1:T(1,128)}, f32[1,158,128]{2,0,1:T(1,128)S(1)}, u32[]{:S(2)}) copy-start(f32[1,158,128]{2,0,1:T(1,128)S(1)} %get-tuple-element.86) | copy-start | bytes 242692
  18.3 58.3 %copy-start.15 = (f32[1,158,128]{2,0,1:T(1,128)}, f32[1,158,128]{2,0,1:T(1,128)S(1)}, u32[]{:S(2)}) copy-start(f32[1,158,128]{2,0,1:T(1,128)S(1)} %get-tuple-element.85) | copy-start | bytes 242692
  28.0 5.8 %collective-permute-start.5 = (f32[15,256]{1,0:T(8,128)S(1)}, f32[15,256]{1,0:T(8,128)S(1)}, u32[]{:S(2)}, u32[]{:S(2)}) collective-permute-start(f32[15,256]{1,0:T(8,128)S(1)} %bitcast.677), channel_id=1, source_target_pairs={{16,0},{32,16},{48,32},{64,48},{80,64},{96,80},{112,96},{17,1},{33... | collective-permute-start | bytes 46088 | tf_op jit(solution)/shard_map/ppermute | solution.py:23
  29.3 5.3 %collective-permute-start.4 = (f32[15,256]{1,0:T(8,128)S(1)}, f32[15,256]{1,0:T(8,128)S(1)}, u32[]{:S(2)}, u32[]{:S(2)}) collective-permute-start(f32[15,256]{1,0:T(8,128)S(1)} %bitcast.674), channel_id=1, source_target_pairs={{0,16},{16,32},{32,48},{48,64},{64,80},{80,96},{96,112},{1,17},{17... | collective-permute-start | bytes 46088 | tf_op jit(solution)/shard_map/ppermute | solution.py:22
  34.7 6.9 %collective-permute-start.7 = (f32[94,15]{1,0:T(8,128)S(1)}, f32[94,15]{1,0:T(8,128)S(1)}, u32[]{:S(2)}, u32[]{:S(2)}) collective-permute-start(f32[94,15]{1,0:T(8,128)S(1)} %get-tuple-element.123), channel_id=1, source_target_pairs={{1,0},{2,1},{3,2},{4,3},{5,4},{6,5},{7,6},{8,7},{9,8},{10,9},{11,1... | collective-permute-start | bytes 16928 | tf_op jit(solution)/shard_map/ppermute | solution.py:23
  36.6 6.0 %collective-permute-start.6 = (f32[94,15]{1,0:T(8,128)S(1)}, f32[94,15]{1,0:T(8,128)S(1)}, u32[]{:S(2)}, u32[]{:S(2)}) collective-permute-start(f32[94,15]{1,0:T(8,128)S(1)} %get-tuple-element.124), channel_id=1, source_target_pairs={{0,1},{1,2},{2,3},{3,4},{4,5},{5,6},{6,7},{7,8},{8,9},{9,10},{10,1... | collective-permute-start | bytes 16928 | tf_op jit(solution)/shard_map/ppermute | solution.py:22
  41.5 56.8 %copy-start.34 = (f32[1,158,128]{2,0,1:T(1,128)}, f32[1,158,128]{2,0,1:T(1,128)S(1)}, u32[]{:S(2)}) copy-start(f32[1,158,128]{2,0,1:T(1,128)S(1)} %get-tuple-element.65) | copy-start | bytes 242692
  41.5 57.1 %copy-start.30 = (f32[1,158,128]{2,0,1:T(1,128)}, f32[1,158,128]{2,0,1:T(1,128)S(1)}, u32[]{:S(2)}) copy-start(f32[1,158,128]{2,0,1:T(1,128)S(1)} %get-tuple-element.64) | copy-start | bytes 242692
  41.5 57.4 %copy-start.24 = (f32[1,158,128]{2,0,1:T(1,128)}, f32[1,158,128]{2,0,1:T(1,128)S(1)}, u32[]{:S(2)}) copy-start(f32[1,158,128]{2,0,1:T(1,128)S(1)} %get-tuple-element.63) | copy-start | bytes 242692
  41.5 57.6 %copy-start.18 = (f32[1,158,128]{2,0,1:T(1,128)}, f32[1,158,128]{2,0,1:T(1,128)S(1)}, u32[]{:S(2)}) copy-start(f32[1,158,128]{2,0,1:T(1,128)S(1)} %get-tuple-element.62) | copy-start | bytes 242692
  41.5 57.9 %copy-start.12 = (f32[1,158,128]{2,0,1:T(1,128)}, f32[1,158,128]{2,0,1:T(1,128)S(1)}, u32[]{:S(2)}) copy-start(f32[1,158,128]{2,0,1:T(1,128)S(1)} %get-tuple-element.61) | copy-start | bytes 242692
  41.5 58.2 %copy-start.9 = (f32[1,158,128]{2,0,1:T(1,128)}, f32[1,158,128]{2,0,1:T(1,128)S(1)}, u32[]{:S(2)}) copy-start(f32[1,158,128]{2,0,1:T(1,128)S(1)} %get-tuple-element.60) | copy-start | bytes 242692
  41.6 58.4 %copy-start.6 = (f32[1,158,128]{2,0,1:T(1,128)}, f32[1,158,128]{2,0,1:T(1,128)S(1)}, u32[]{:S(2)}) copy-start(f32[1,158,128]{2,0,1:T(1,128)S(1)} %get-tuple-element.59) | copy-start | bytes 242692
  41.6 58.7 %copy-start.3 = (f32[1,158,128]{2,0,1:T(1,128)}, f32[1,158,128]{2,0,1:T(1,128)S(1)}, u32[]{:S(2)}) copy-start(f32[1,158,128]{2,0,1:T(1,128)S(1)} %get-tuple-element.58) | copy-start | bytes 242692
  41.6 59.0 %copy-start = (f32[1,158,128]{2,0,1:T(1,128)}, f32[1,158,128]{2,0,1:T(1,128)S(1)}, u32[]{:S(2)}) copy-start(f32[1,158,128]{2,0,1:T(1,128)S(1)} %get-tuple-element.57) | copy-start | bytes 242692
  51.3 5.2 %collective-permute-start.8 = (f32[15,256]{1,0:T(8,128)S(1)}, f32[15,256]{1,0:T(8,128)S(1)}, u32[]{:S(2)}, u32[]{:S(2)}) collective-permute-start(f32[15,256]{1,0:T(8,128)S(1)} %get-tuple-element.141), channel_id=1, source_target_pairs={{0,16},{16,32},{32,48},{48,64},{64,80},{80,96},{96,112},{1,17},{17... | collective-permute-start | bytes 46088 | tf_op jit(solution)/shard_map/ppermute | solution.py:22
  55.2 6.0 %collective-permute-start.9 = (f32[15,256]{1,0:T(8,128)S(1)}, f32[15,256]{1,0:T(8,128)S(1)}, u32[]{:S(2)}, u32[]{:S(2)}) collective-permute-start(f32[15,256]{1,0:T(8,128)S(1)} %get-tuple-element.142), channel_id=1, source_target_pairs={{16,0},{32,16},{48,32},{64,48},{80,64},{96,80},{112,96},{17,1},{33... | collective-permute-start | bytes 46088 | tf_op jit(solution)/shard_map/ppermute | solution.py:23
  61.3 6.1 %collective-permute-start.10 = (f32[94,15]{1,0:T(8,128)S(1)}, f32[94,15]{1,0:T(8,128)S(1)}, u32[]{:S(2)}, u32[]{:S(2)}) collective-permute-start(f32[94,15]{1,0:T(8,128)S(1)} %get-tuple-element.119), channel_id=1, source_target_pairs={{0,1},{1,2},{2,3},{3,4},{4,5},{5,6},{6,7},{7,8},{8,9},{9,10},{10,1... | collective-permute-start | bytes 16928 | tf_op jit(solution)/shard_map/ppermute | solution.py:22
  65.3 8.0 %collective-permute-start.11 = (f32[94,15]{1,0:T(8,128)S(1)}, f32[94,15]{1,0:T(8,128)S(1)}, u32[]{:S(2)}, u32[]{:S(2)}) collective-permute-start(f32[94,15]{1,0:T(8,128)S(1)} %get-tuple-element.120), channel_id=1, source_target_pairs={{1,0},{2,1},{3,2},{4,3},{5,4},{6,5},{7,6},{8,7},{9,8},{10,9},{11,1... | collective-permute-start | bytes 16928 | tf_op jit(solution)/shard_map/ppermute | solution.py:23
  82.1 5.2 %collective-permute-start.13 = (f32[15,256]{1,0:T(8,128)S(1)}, f32[15,256]{1,0:T(8,128)S(1)}, u32[]{:S(2)}, u32[]{:S(2)}) collective-permute-start(f32[15,256]{1,0:T(8,128)S(1)} %bitcast.678), channel_id=1, source_target_pairs={{16,0},{32,16},{48,32},{64,48},{80,64},{96,80},{112,96},{17,1},{33... | collective-permute-start | bytes 46088 | tf_op jit(solution)/shard_map/ppermute | solution.py:23
  83.4 4.7 %collective-permute-start.12 = (f32[15,256]{1,0:T(8,128)S(1)}, f32[15,256]{1,0:T(8,128)S(1)}, u32[]{:S(2)}, u32[]{:S(2)}) collective-permute-start(f32[15,256]{1,0:T(8,128)S(1)} %bitcast.675), channel_id=1, source_target_pairs={{0,16},{16,32},{32,48},{48,64},{64,80},{80,96},{96,112},{1,17},{17... | collective-permute-start | bytes 46088 | tf_op jit(solution)/shard_map/ppermute | solution.py:22
  88.1 8.6 %collective-permute-start.15 = (f32[94,15]{1,0:T(8,128)S(1)}, f32[94,15]{1,0:T(8,128)S(1)}, u32[]{:S(2)}, u32[]{:S(2)}) collective-permute-start(f32[94,15]{1,0:T(8,128)S(1)} %get-tuple-element.115), channel_id=1, source_target_pairs={{1,0},{2,1},{3,2},{4,3},{5,4},{6,5},{7,6},{8,7},{9,8},{10,9},{11,1... | collective-permute-start | bytes 16928 | tf_op jit(solution)/shard_map/ppermute | solution.py:23
  90.1 8.1 %collective-permute-start.14 = (f32[94,15]{1,0:T(8,128)S(1)}, f32[94,15]{1,0:T(8,128)S(1)}, u32[]{:S(2)}, u32[]{:S(2)}) collective-permute-start(f32[94,15]{1,0:T(8,128)S(1)} %get-tuple-element.116), channel_id=1, source_target_pairs={{0,1},{1,2},{2,3},{3,4},{4,5},{5,6},{6,7},{7,8},{8,9},{9,10},{10,1... | collective-permute-start | bytes 16928 | tf_op jit(solution)/shard_map/ppermute | solution.py:22
  107.6 70.8 %copy-start.47 = (f32[64,256]{1,0:T(8,128)}, f32[64,256]{1,0:T(8,128)S(1)}, u32[]{:S(2)}) copy-start(f32[64,256]{1,0:T(8,128)S(1)} %get-tuple-element.34) | copy-start | bytes 196612
  155.2 2.6 collective-permute-start.16
  156.5 3.1 collective-permute-start.17
  159.7 6.5 %collective-permute-start.18 = (f32[94,15]{1,0:T(8,128)S(1)}, f32[94,15]{1,0:T(8,128)S(1)}, u32[]{:S(2)}, u32[]{:S(2)}) collective-permute-start(f32[94,15]{1,0:T(8,128)S(1)} %get-tuple-element.111), channel_id=1, source_target_pairs={{0,1},{1,2},{2,3},{3,4},{4,5},{5,6},{6,7},{7,8},{8,9},{9,10},{10,1... | collective-permute-start | bytes 16928 | tf_op jit(solution)/shard_map/ppermute | solution.py:22
  161.6 6.1 %collective-permute-start.19 = (f32[94,15]{1,0:T(8,128)S(1)}, f32[94,15]{1,0:T(8,128)S(1)}, u32[]{:S(2)}, u32[]{:S(2)}) collective-permute-start(f32[94,15]{1,0:T(8,128)S(1)} %get-tuple-element.112), channel_id=1, source_target_pairs={{1,0},{2,1},{3,2},{4,3},{5,4},{6,5},{7,6},{8,7},{9,8},{10,9},{11,1... | collective-permute-start | bytes 16928 | tf_op jit(solution)/shard_map/ppermute | solution.py:23
  184.5 4.5 %collective-permute-start.21 = (f32[15,256]{1,0:T(8,128)S(1)}, f32[15,256]{1,0:T(8,128)S(1)}, u32[]{:S(2)}, u32[]{:S(2)}) collective-permute-start(f32[15,256]{1,0:T(8,128)S(1)} %bitcast.679), channel_id=1, source_target_pairs={{16,0},{32,16},{48,32},{64,48},{80,64},{96,80},{112,96},{17,1},{33... | collective-permute-start | bytes 46088 | tf_op jit(solution)/shard_map/ppermute | solution.py:23
  185.8 4.1 %collective-permute-start.20 = (f32[15,256]{1,0:T(8,128)S(1)}, f32[15,256]{1,0:T(8,128)S(1)}, u32[]{:S(2)}, u32[]{:S(2)}) collective-permute-start(f32[15,256]{1,0:T(8,128)S(1)} %bitcast.676), channel_id=1, source_target_pairs={{0,16},{16,32},{32,48},{48,64},{64,80},{80,96},{96,112},{1,17},{17... | collective-permute-start | bytes 46088 | tf_op jit(solution)/shard_map/ppermute | solution.py:22
  190.0 6.0 %collective-permute-start.23 = (f32[94,15]{1,0:T(8,128)S(1)}, f32[94,15]{1,0:T(8,128)S(1)}, u32[]{:S(2)}, u32[]{:S(2)}) collective-permute-start(f32[94,15]{1,0:T(8,128)S(1)} %get-tuple-element.107), channel_id=1, source_target_pairs={{1,0},{2,1},{3,2},{4,3},{5,4},{6,5},{7,6},{8,7},{9,8},{10,9},{11,1... | collective-permute-start | bytes 16928 | tf_op jit(solution)/shard_map/ppermute | solution.py:23
  193.7 6.1 %collective-permute-start.22 = (f32[94,15]{1,0:T(8,128)S(1)}, f32[94,15]{1,0:T(8,128)S(1)}, u32[]{:S(2)}, u32[]{:S(2)}) collective-permute-start(f32[94,15]{1,0:T(8,128)S(1)} %get-tuple-element.108), channel_id=1, source_target_pairs={{0,1},{1,2},{2,3},{3,4},{4,5},{5,6},{6,7},{7,8},{8,9},{9,10},{10,1... | collective-permute-start | bytes 16928 | tf_op jit(solution)/shard_map/ppermute | solution.py:22
  253.7 2.6 collective-permute-start.24
  255.0 3.7 %collective-permute-start.25 = (f32[15,256]{1,0:T(8,128)S(1)}, f32[15,256]{1,0:T(8,128)S(1)}, u32[]{:S(2)}, u32[]{:S(2)}) collective-permute-start(f32[15,256]{1,0:T(8,128)S(1)} %get-tuple-element.134), channel_id=1, source_target_pairs={{16,0},{32,16},{48,32},{64,48},{80,64},{96,80},{112,96},{17,1},{33... | collective-permute-start | bytes 46088 | tf_op jit(solution)/shard_map/ppermute | solution.py:23
  258.8 6.2 %collective-permute-start.26 = (f32[94,15]{1,0:T(8,128)S(1)}, f32[94,15]{1,0:T(8,128)S(1)}, u32[]{:S(2)}, u32[]{:S(2)}) collective-permute-start(f32[94,15]{1,0:T(8,128)S(1)} %get-tuple-element.103), channel_id=1, source_target_pairs={{0,1},{1,2},{2,3},{3,4},{4,5},{5,6},{6,7},{7,8},{8,9},{9,10},{10,1... | collective-permute-start | bytes 16928 | tf_op jit(solution)/shard_map/ppermute | solution.py:22
  260.7 6.1 %collective-permute-start.27 = (f32[94,15]{1,0:T(8,128)S(1)}, f32[94,15]{1,0:T(8,128)S(1)}, u32[]{:S(2)}, u32[]{:S(2)}) collective-permute-start(f32[94,15]{1,0:T(8,128)S(1)} %get-tuple-element.104), channel_id=1, source_target_pairs={{1,0},{2,1},{3,2},{4,3},{5,4},{6,5},{7,6},{8,7},{9,8},{10,9},{11,1... | collective-permute-start | bytes 16928 | tf_op jit(solution)/shard_map/ppermute | solution.py:23
  283.6 5.2 %collective-permute-start.29 = (f32[15,256]{1,0:T(8,128)S(1)}, f32[15,256]{1,0:T(8,128)S(1)}, u32[]{:S(2)}, u32[]{:S(2)}) collective-permute-start(f32[15,256]{1,0:T(8,128)S(1)} %bitcast.680), channel_id=1, source_target_pairs={{16,0},{32,16},{48,32},{64,48},{80,64},{96,80},{112,96},{17,1},{33... | collective-permute-start | bytes 46088 | tf_op jit(solution)/shard_map/ppermute | solution.py:23
  284.9 4.7 %collective-permute-start.28 = (f32[15,256]{1,0:T(8,128)S(1)}, f32[15,256]{1,0:T(8,128)S(1)}, u32[]{:S(2)}, u32[]{:S(2)}) collective-permute-start(f32[15,256]{1,0:T(8,128)S(1)} %bitcast.673), channel_id=1, source_target_pairs={{0,16},{16,32},{32,48},{48,64},{64,80},{80,96},{96,112},{1,17},{17... | collective-permute-start | bytes 46088 | tf_op jit(solution)/shard_map/ppermute | solution.py:22
  289.7 6.1 %collective-permute-start.31 = (f32[94,15]{1,0:T(8,128)S(1)}, f32[94,15]{1,0:T(8,128)S(1)}, u32[]{:S(2)}, u32[]{:S(2)}) collective-permute-start(f32[94,15]{1,0:T(8,128)S(1)} %get-tuple-element.99), channel_id=1, source_target_pairs={{1,0},{2,1},{3,2},{4,3},{5,4},{6,5},{7,6},{8,7},{9,8},{10,9},{11,1... | collective-permute-start | bytes 16928 | tf_op jit(solution)/shard_map/ppermute | solution.py:23
  293.4 6.0 %collective-permute-start.30 = (f32[94,15]{1,0:T(8,128)S(1)}, f32[94,15]{1,0:T(8,128)S(1)}, u32[]{:S(2)}, u32[]{:S(2)}) collective-permute-start(f32[94,15]{1,0:T(8,128)S(1)} %get-tuple-element.100), channel_id=1, source_target_pairs={{0,1},{1,2},{2,3},{3,4},{4,5},{5,6},{6,7},{7,8},{8,9},{9,10},{10,1... | collective-permute-start | bytes 16928 | tf_op jit(solution)/shard_map/ppermute | solution.py:22
  (35 other events, 939.7 us)
where the time goes:
time: 360 us; the launch traced here: 353 us
  blocking collectives  125 us (35%)
  starting transfers between devices  85.5 us (24%)
  matrix products  84.5 us (23%)
  waiting for transfers between devices  32 us (9%)
  between operations  13.6 us (4%)
  local copies, waits for them, and re-layouts  7.13 us (2%)
  other arithmetic  5.84 us (2%)
    psum x12, blocking collectives, one_axis_at_a_time(): x = lax.psum(x, axis)  125 us
    dot_general x248, matrix products, correlate(): jnp.einsum('rnk,kj->rnj', window, tables[shift_row], precision=lax.Precis...  81.2 us
    ppermute x16, starting transfers between devices, with_halo(): before = lax.ppermute(last, axis, up)  51 us
    ppermute x16, starting transfers between devices, with_halo(): after = lax.ppermute(initial, axis, down)  34.4 us
    ppermute x16, waiting for transfers between devices, with_halo(): after = lax.ppermute(initial, axis, down)  18.1 us
    ppermute x16, waiting for transfers between devices, with_halo(): before = lax.ppermute(last, axis, up)  13.9 us
  transfers between devices with their start and end apart: 32, of which 15 were waited for; matrix products, arithmetic and copies ran while one was open for 2% of the time, Pallas kernels for 0%

commit v1 on v0

--- a/solution.py
+++ b/solution.py
@@ -27,7 +27,8 @@
 
 def one_axis_at_a_time(x, axes):
     for axis in axes:
-        x = lax.psum(x, axis)
+        parts = lax.all_gather(x, axis, axis=0, tiled=False)
+        x = parts.sum(axis=0)
     return x
 
 

time: 360 us -> 414 us (1.15)
  local copies, waits for them, and re-layouts: 7.13 us -> 44.1 us
  other arithmetic: 5.84 us -> 21.7 us
  matrix products: 84.5 us -> 92.5 us
  blocking collectives: 125 us -> 117 us
    psum x12 -> x0, blocking collectives: 125 us -> none  [one_axis_at_a_time(): x = lax.psum(x, axis)]
    unnamed x0 -> x12, blocking collectives: none -> 117 us
    unnamed x118 -> x188, local copies, waits for them, and re-layouts: 0.32 us -> 36.6 us
    reduce_sum x0 -> x24, other arithmetic: none -> 15.1 us  [one_axis_at_a_time(): x = parts.sum(axis=0)]
    dot_general x248, matrix products: 81.2 us -> 89.1 us  [correlate(): jnp.einsum('rnk,kj->rnj', window, tables[shift_row], precision=lax.Precis...]
where the time goes in v1:
time: 414 us; the launch traced here: 407 us
  blocking collectives  117 us (28%)
  matrix products  92.5 us (22%)
  starting transfers between devices  85.4 us (21%)
  local copies, waits for them, and re-layouts  44.1 us (11%)
  waiting for transfers between devices  31.9 us (8%)
  other arithmetic  21.7 us (5%)
  between operations  14.1 us (3%)
    unnamed x12, blocking collectives  117 us
    dot_general x248, matrix products, correlate(): jnp.einsum('rnk,kj->rnj', window, tables[shift_row], precision=lax.Precis...  89.1 us
    ppermute x16, starting transfers between devices, with_halo(): before = lax.ppermute(last, axis, up)  51.2 us
    unnamed x188, local copies, waits for them, and re-layouts  36.6 us
    ppermute x16, starting transfers between devices, with_halo(): after = lax.ppermute(initial, axis, down)  34.2 us
    ppermute x16, waiting for transfers between devices, with_halo(): after = lax.ppermute(initial, axis, down)  18.4 us
    reduce_sum x24, other arithmetic, one_axis_at_a_time(): x = parts.sum(axis=0)  15.1 us
    ppermute x16, waiting for transfers between devices, with_halo(): before = lax.ppermute(last, axis, up)  13.5 us
  transfers between devices with their start and end apart: 32, of which 15 were waited for; matrix products, arithmetic and copies ran while one was open for 2% of the time, Pallas kernels for 0%

profile of v1, /device:TPU:2, one launch (start us, length us, event | category | flops | bytes accessed | tf_op | source)
XLA Modules:
  0.0 406.5 jit_solution(6838787012146748974)
XLA Ops:
  1.4 1.7 collective-permute-start
  5.2 2.0 fusion.2
  11.4 1.9 collective-permute-start.3
  13.4 4.1 %collective-permute-start.2 = (f32[94,15]{1,0:T(8,128)S(1)}, f32[94,15]{1,0:T(8,128)S(1)}, u32[]{:S(2)}, u32[]{:S(2)}) collective-permute-start(f32[94,15]{1,0:T(8,128)S(1)} %get-tuple-element.128), channel_id=1, source_target_pairs={{0,1},{1,2},{2,3},{3,4},{4,5},{5,6},{6,7},{7,8},{8,9},{9,10},{10,1... | collective-permute-start | bytes 16928 | tf_op jit(solution)/shard_map/ppermute | solution.py:22
  29.3 4.5 %collective-permute-start.4 = (f32[15,256]{1,0:T(8,128)S(1)}, f32[15,256]{1,0:T(8,128)S(1)}, u32[]{:S(2)}, u32[]{:S(2)}) collective-permute-start(f32[15,256]{1,0:T(8,128)S(1)} %bitcast.701), channel_id=1, source_target_pairs={{0,16},{16,32},{32,48},{48,64},{64,80},{80,96},{96,112},{1,17},{17... | collective-permute-start | bytes 46088 | tf_op jit(solution)/shard_map/ppermute | solution.py:22
  34.7 1.9 collective-permute-start.7
  36.6 4.1 %collective-permute-start.6 = (f32[94,15]{1,0:T(8,128)S(1)}, f32[94,15]{1,0:T(8,128)S(1)}, u32[]{:S(2)}, u32[]{:S(2)}) collective-permute-start(f32[94,15]{1,0:T(8,128)S(1)} %get-tuple-element.124), channel_id=1, source_target_pairs={{0,1},{1,2},{2,3},{3,4},{4,5},{5,6},{6,7},{7,8},{8,9},{9,10},{10,1... | collective-permute-start | bytes 16928 | tf_op jit(solution)/shard_map/ppermute | solution.py:22
  51.3 3.9 collective-permute-start.8
  56.6 4.7 %collective-permute-done.9 = f32[15,256]{1,0:T(8,128)S(1)} collective-permute-done((f32[15,256]{1,0:T(8,128)S(1)}, f32[15,256]{1,0:T(8,128)S(1)}, u32[]{:S(2)}, u32[]{:S(2)}) %collective-permute-start.9) | collective-permute-done | bytes 15392 | tf_op jit(solution)/shard_map/ppermute | solution.py:23
  61.4 3.9 collective-permute-start.10
  65.3 2.2 collective-permute-start.11
  67.5 5.8 %collective-permute-done.11 = f32[94,15]{1,0:T(8,128)S(1)} collective-permute-done((f32[94,15]{1,0:T(8,128)S(1)}, f32[94,15]{1,0:T(8,128)S(1)}, u32[]{:S(2)}, u32[]{:S(2)}) %collective-permute-start.11) | collective-permute-done | bytes 5672 | tf_op jit(solution)/shard_map/ppermute | solution.py:23
  83.9 3.9 collective-permute-start.12
  89.3 1.9 collective-permute-start.15
  91.3 6.8 %collective-permute-start.14 = (f32[94,15]{1,0:T(8,128)}, f32[94,15]{1,0:T(8,128)}, u32[]{:S(2)}, u32[]{:S(2)}) collective-permute-start(f32[94,15]{1,0:T(8,128)} %get-tuple-element.116), channel_id=1, source_target_pairs={{0,1},{1,2},{2,3},{3,4},{4,5},{5,6},{6,7},{7,8},{8,9},{9,10},{10,1... | collective-permute-start | bytes 16928 | tf_op jit(solution)/shard_map/ppermute | solution.py:22
  121.6 13.8 %all-reduce.32 = (f32[4]{0:T(128)S(1)}, f32[4]{0:T(128)S(1)}) all-reduce(f32[4]{0:T(128)S(1)} %dynamic-update-slice, f32[4]{0:T(128)S(1)} %dynamic-update-slice.4), channel_id=1, replica_groups=mesh['row_0'=4,'row_1'=2,'col_0'=4,'col_1'=4] {'row_0'}, use_global_device_ids=true, to_apply=%add | all-reduce | flops 8 | bytes 64
  137.8 1.4 dynamic-update-slice.1
  140.5 2.4 all-reduce.35
  145.3 1.4 dynamic-update-slice.2
  147.9 15.8 %all-reduce.29 = (f32[4]{0:T(128)S(1)}, f32[4]{0:T(128)S(1)}) all-reduce(f32[4]{0:T(128)S(1)} %dynamic-update-slice.2, f32[4]{0:T(128)S(1)} %dynamic-update-slice.6), channel_id=1, replica_groups=mesh['row_0'=4,'row_1'=2,'col_0'=4,'col_1'=4] {'col_0'}, use_global_device_ids=true, to_apply=%add.2 | all-reduce | flops 8 | bytes 64
  167.5 11.8 %all-reduce.26 = (f32[4]{0:T(128)S(1)}, f32[4]{0:T(128)S(1)}) all-reduce(f32[4]{0:T(128)S(1)} %dynamic-update-slice.3, f32[4]{0:T(128)S(1)} %dynamic-update-slice.7), channel_id=1, replica_groups=mesh['row_0'=4,'row_1'=2,'col_0'=4,'col_1'=4] {'col_1'}, use_global_device_ids=true, to_apply=%add.3 | all-reduce | flops 8 | bytes 64
  184.5 1.8 collective-permute-done.17
  186.4 1.9 collective-permute-start.18
  188.3 4.2 %collective-permute-start.19 = (f32[94,15]{1,0:T(8,128)S(1)}, f32[94,15]{1,0:T(8,128)S(1)}, u32[]{:S(2)}, u32[]{:S(2)}) collective-permute-start(f32[94,15]{1,0:T(8,128)S(1)} %get-tuple-element.112), channel_id=1, source_target_pairs={{1,0},{2,1},{3,2},{4,3},{5,4},{6,5},{7,6},{8,7},{9,8},{10,9},{11,1... | collective-permute-start | bytes 16928 | tf_op jit(solution)/shard_map/ppermute | solution.py:23
  192.6 1.9 collective-permute-done.19
  212.6 3.2 collective-permute-start.20
  216.7 3.7 collective-permute-start.23
  220.4 2.3 collective-permute-start.22
  222.8 3.8 collective-permute-done.22
  235.1 1.4 multiply_reduce_fusion.2
  239.1 12.1 %all-reduce.31 = (f32[4]{0:T(128)S(1)}, f32[4]{0:T(128)S(1)}) all-reduce(f32[4]{0:T(128)S(1)} %dynamic-update-slice.8, f32[4]{0:T(128)S(1)} %dynamic-update-slice.12), channel_id=1, replica_groups=mesh['row_0'=4,'row_1'=2,'col_0'=4,'col_1'=4] {'row_0'}, use_global_device_ids=true, to_apply=%add.8 | all-reduce | flops 8 | bytes 64
  251.8 1.4 dynamic-update-slice.13
  253.9 1.4 dynamic-update-slice.9
  255.2 2.4 all-reduce.34
  261.7 9.7 %all-reduce.28 = (f32[4]{0:T(128)S(1)}, f32[4]{0:T(128)S(1)}) all-reduce(f32[4]{0:T(128)S(1)} %dynamic-update-slice.10, f32[4]{0:T(128)S(1)} %dynamic-update-slice.14), channel_id=1, replica_groups=mesh['row_0'=4,'row_1'=2,'col_0'=4,'col_1'=4] {'col_0'}, use_global_device_ids=true, to_apply=%add.10 | all-reduce | flops 8 | bytes 64
  275.2 11.8 %all-reduce.25 = (f32[4]{0:T(128)S(1)}, f32[4]{0:T(128)S(1)}) all-reduce(f32[4]{0:T(128)S(1)} %dynamic-update-slice.11, f32[4]{0:T(128)S(1)} %dynamic-update-slice.15), channel_id=1, replica_groups=mesh['row_0'=4,'row_1'=2,'col_0'=4,'col_1'=4] {'col_1'}, use_global_device_ids=true, to_apply=%add.11 | all-reduce | flops 8 | bytes 64
  296.3 2.4 collective-permute-done.25
  298.8 1.9 collective-permute-start.26
  300.8 4.3 %collective-permute-start.27 = (f32[94,15]{1,0:T(8,128)S(1)}, f32[94,15]{1,0:T(8,128)S(1)}, u32[]{:S(2)}, u32[]{:S(2)}) collective-permute-start(f32[94,15]{1,0:T(8,128)S(1)} %get-tuple-element.104), channel_id=1, source_target_pairs={{1,0},{2,1},{3,2},{4,3},{5,4},{6,5},{7,6},{8,7},{9,8},{10,9},{11,1... | collective-permute-start | bytes 16928 | tf_op jit(solution)/shard_map/ppermute | solution.py:23
  305.1 1.8 collective-permute-done.27
  325.0 3.9 collective-permute-start.28
  329.7 3.7 collective-permute-start.31
  333.4 2.5 collective-permute-start.30
  335.9 3.5 collective-permute-done.30
  351.3 12.3 %all-reduce.30 = (f32[4]{0:T(128)S(1)}, f32[4]{0:T(128)S(1)}) all-reduce(f32[4]{0:T(128)S(1)} %dynamic-update-slice.16, f32[4]{0:T(128)S(1)} %dynamic-update-slice.20), channel_id=1, replica_groups=mesh['row_0'=4,'row_1'=2,'col_0'=4,'col_1'=4] {'row_0'}, use_global_device_ids=true, to_apply=%add.16 | all-reduce | flops 8 | bytes 64
  367.7 2.4 all-reduce.33
  374.2 10.6 %all-reduce.27 = (f32[4]{0:T(128)S(1)}, f32[4]{0:T(128)S(1)}) all-reduce(f32[4]{0:T(128)S(1)} %dynamic-update-slice.18, f32[4]{0:T(128)S(1)} %dynamic-update-slice.22), channel_id=1, replica_groups=mesh['row_0'=4,'row_1'=2,'col_0'=4,'col_1'=4] {'col_0'}, use_global_device_ids=true, to_apply=%add.18 | all-reduce | flops 8 | bytes 64
  388.5 11.8 %all-reduce.24 = (f32[4]{0:T(128)S(1)}, f32[4]{0:T(128)S(1)}) all-reduce(f32[4]{0:T(128)S(1)} %dynamic-update-slice.19, f32[4]{0:T(128)S(1)} %dynamic-update-slice.23), channel_id=1, replica_groups=mesh['row_0'=4,'row_1'=2,'col_0'=4,'col_1'=4] {'col_1'}, use_global_device_ids=true, to_apply=%add.19 | all-reduce | flops 8 | bytes 64
  (554 shorter events, 168.4 us)
Async XLA Ops:
  1.4 9.9 %collective-permute-start = (f32[15,256]{1,0:T(8,128)S(1)}, f32[15,256]{1,0:T(8,128)S(1)}, u32[]{:S(2)}, u32[]{:S(2)}) collective-permute-start(f32[15,256]{1,0:T(8,128)S(1)} %get-tuple-element.145), channel_id=1, source_target_pairs={{0,16},{16,32},{32,48},{48,64},{64,80},{80,96},{96,112},{1,17},{17... | collective-permute-start | bytes 46088 | tf_op jit(solution)/shard_map/ppermute | solution.py:22
  3.1 8.2 %collective-permute-start.1 = (f32[15,256]{1,0:T(8,128)S(1)}, f32[15,256]{1,0:T(8,128)S(1)}, u32[]{:S(2)}, u32[]{:S(2)}) collective-permute-start(f32[15,256]{1,0:T(8,128)S(1)} %get-tuple-element.146), channel_id=1, source_target_pairs={{16,0},{32,16},{48,32},{64,48},{80,64},{96,80},{112,96},{17,1},{33... | collective-permute-start | bytes 46088 | tf_op jit(solution)/shard_map/ppermute | solution.py:23
  11.4 6.9 %collective-permute-start.3 = (f32[94,15]{1,0:T(8,128)S(1)}, f32[94,15]{1,0:T(8,128)S(1)}, u32[]{:S(2)}, u32[]{:S(2)}) collective-permute-start(f32[94,15]{1,0:T(8,128)S(1)} %get-tuple-element.127), channel_id=1, source_target_pairs={{1,0},{2,1},{3,2},{4,3},{5,4},{6,5},{7,6},{8,7},{9,8},{10,9},{11,1... | collective-permute-start | bytes 16928 | tf_op jit(solution)/shard_map/ppermute | solution.py:23
  13.4 6.0 %collective-permute-start.2 = (f32[94,15]{1,0:T(8,128)S(1)}, f32[94,15]{1,0:T(8,128)S(1)}, u32[]{:S(2)}, u32[]{:S(2)}) collective-permute-start(f32[94,15]{1,0:T(8,128)S(1)} %get-tuple-element.128), channel_id=1, source_target_pairs={{0,1},{1,2},{2,3},{3,4},{4,5},{5,6},{6,7},{7,8},{8,9},{9,10},{10,1... | collective-permute-start | bytes 16928 | tf_op jit(solution)/shard_map/ppermute | solution.py:22
  18.2 55.8 %copy-start.44 = (f32[1,158,128]{2,0,1:T(1,128)}, f32[1,158,128]{2,0,1:T(1,128)S(1)}, u32[]{:S(2)}) copy-start(f32[1,158,128]{2,0,1:T(1,128)S(1)} %get-tuple-element.96) | copy-start | bytes 242692
  18.2 56.1 %copy-start.43 = (f32[1,158,128]{2,0,1:T(1,128)}, f32[1,158,128]{2,0,1:T(1,128)S(1)}, u32[]{:S(2)}) copy-start(f32[1,158,128]{2,0,1:T(1,128)S(1)} %get-tuple-element.95) | copy-start | bytes 242692
  18.2 56.3 %copy-start.42 = (f32[1,158,128]{2,0,1:T(1,128)}, f32[1,158,128]{2,0,1:T(1,128)S(1)}, u32[]{:S(2)}) copy-start(f32[1,158,128]{2,0,1:T(1,128)S(1)} %get-tuple-element.94) | copy-start | bytes 242692
  18.2 56.6 %copy-start.41 = (f32[1,158,128]{2,0,1:T(1,128)}, f32[1,158,128]{2,0,1:T(1,128)S(1)}, u32[]{:S(2)}) copy-start(f32[1,158,128]{2,0,1:T(1,128)S(1)} %get-tuple-element.93) | copy-start | bytes 242692
  18.3 56.9 %copy-start.40 = (f32[1,158,128]{2,0,1:T(1,128)}, f32[1,158,128]{2,0,1:T(1,128)S(1)}, u32[]{:S(2)}) copy-start(f32[1,158,128]{2,0,1:T(1,128)S(1)} %get-tuple-element.92) | copy-start | bytes 242692
  18.3 57.2 %copy-start.39 = (f32[1,158,128]{2,0,1:T(1,128)}, f32[1,158,128]{2,0,1:T(1,128)S(1)}, u32[]{:S(2)}) copy-start(f32[1,158,128]{2,0,1:T(1,128)S(1)} %get-tuple-element.91) | copy-start | bytes 242692
  18.3 57.4 %copy-start.38 = (f32[1,158,128]{2,0,1:T(1,128)}, f32[1,158,128]{2,0,1:T(1,128)S(1)}, u32[]{:S(2)}) copy-start(f32[1,158,128]{2,0,1:T(1,128)S(1)} %get-tuple-element.90) | copy-start | bytes 242692
  18.3 57.7 %copy-start.37 = (f32[1,158,128]{2,0,1:T(1,128)}, f32[1,158,128]{2,0,1:T(1,128)S(1)}, u32[]{:S(2)}) copy-start(f32[1,158,128]{2,0,1:T(1,128)S(1)} %get-tuple-element.89) | copy-start | bytes 242692
  18.3 58.0 %copy-start.30 = (f32[1,158,128]{2,0,1:T(1,128)}, f32[1,158,128]{2,0,1:T(1,128)S(1)}, u32[]{:S(2)}) copy-start(f32[1,158,128]{2,0,1:T(1,128)S(1)} %get-tuple-element.88) | copy-start | bytes 242692
  18.3 58.2 %copy-start.24 = (f32[1,158,128]{2,0,1:T(1,128)}, f32[1,158,128]{2,0,1:T(1,128)S(1)}, u32[]{:S(2)}) copy-start(f32[1,158,128]{2,0,1:T(1,128)S(1)} %get-tuple-element.87) | copy-start | bytes 242692
  18.3 58.5 %copy-start.18 = (f32[1,158,128]{2,0,1:T(1,128)}, f32[1,158,128]{2,0,1:T(1,128)S(1)}, u32[]{:S(2)}) copy-start(f32[1,158,128]{2,0,1:T(1,128)S(1)} %get-tuple-element.86) | copy-start | bytes 242692
  18.3 58.8 %copy-start.12 = (f32[1,158,128]{2,0,1:T(1,128)}, f32[1,158,128]{2,0,1:T(1,128)S(1)}, u32[]{:S(2)}) copy-start(f32[1,158,128]{2,0,1:T(1,128)S(1)} %get-tuple-element.85) | copy-start | bytes 242692
  28.0 5.8 %collective-permute-start.5 = (f32[15,256]{1,0:T(8,128)S(1)}, f32[15,256]{1,0:T(8,128)S(1)}, u32[]{:S(2)}, u32[]{:S(2)}) collective-permute-start(f32[15,256]{1,0:T(8,128)S(1)} %bitcast.705), channel_id=1, source_target_pairs={{16,0},{32,16},{48,32},{64,48},{80,64},{96,80},{112,96},{17,1},{33... | collective-permute-start | bytes 46088 | tf_op jit(solution)/shard_map/ppermute | solution.py:23
  29.3 5.3 %collective-permute-start.4 = (f32[15,256]{1,0:T(8,128)S(1)}, f32[15,256]{1,0:T(8,128)S(1)}, u32[]{:S(2)}, u32[]{:S(2)}) collective-permute-start(f32[15,256]{1,0:T(8,128)S(1)} %bitcast.701), channel_id=1, source_target_pairs={{0,16},{16,32},{32,48},{48,64},{64,80},{80,96},{96,112},{1,17},{17... | collective-permute-start | bytes 46088 | tf_op jit(solution)/shard_map/ppermute | solution.py:22
  34.7 6.9 %collective-permute-start.7 = (f32[94,15]{1,0:T(8,128)S(1)}, f32[94,15]{1,0:T(8,128)S(1)}, u32[]{:S(2)}, u32[]{:S(2)}) collective-permute-start(f32[94,15]{1,0:T(8,128)S(1)} %get-tuple-element.123), channel_id=1, source_target_pairs={{1,0},{2,1},{3,2},{4,3},{5,4},{6,5},{7,6},{8,7},{9,8},{10,9},{11,1... | collective-permute-start | bytes 16928 | tf_op jit(solution)/shard_map/ppermute | solution.py:23
  36.6 6.0 %collective-permute-start.6 = (f32[94,15]{1,0:T(8,128)S(1)}, f32[94,15]{1,0:T(8,128)S(1)}, u32[]{:S(2)}, u32[]{:S(2)}) collective-permute-start(f32[94,15]{1,0:T(8,128)S(1)} %get-tuple-element.124), channel_id=1, source_target_pairs={{0,1},{1,2},{2,3},{3,4},{4,5},{5,6},{6,7},{7,8},{8,9},{9,10},{10,1... | collective-permute-start | bytes 16928 | tf_op jit(solution)/shard_map/ppermute | solution.py:22
  51.3 5.2 %collective-permute-start.8 = (f32[15,256]{1,0:T(8,128)S(1)}, f32[15,256]{1,0:T(8,128)S(1)}, u32[]{:S(2)}, u32[]{:S(2)}) collective-permute-start(f32[15,256]{1,0:T(8,128)S(1)} %get-tuple-element.141), channel_id=1, source_target_pairs={{0,16},{16,32},{32,48},{48,64},{64,80},{80,96},{96,112},{1,17},{17... | collective-permute-start | bytes 46088 | tf_op jit(solution)/shard_map/ppermute | solution.py:22
  55.3 6.0 %collective-permute-start.9 = (f32[15,256]{1,0:T(8,128)S(1)}, f32[15,256]{1,0:T(8,128)S(1)}, u32[]{:S(2)}, u32[]{:S(2)}) collective-permute-start(f32[15,256]{1,0:T(8,128)S(1)} %get-tuple-element.142), channel_id=1, source_target_pairs={{16,0},{32,16},{48,32},{64,48},{80,64},{96,80},{112,96},{17,1},{33... | collective-permute-start | bytes 46088 | tf_op jit(solution)/shard_map/ppermute | solution.py:23
  61.4 6.1 %collective-permute-start.10 = (f32[94,15]{1,0:T(8,128)S(1)}, f32[94,15]{1,0:T(8,128)S(1)}, u32[]{:S(2)}, u32[]{:S(2)}) collective-permute-start(f32[94,15]{1,0:T(8,128)S(1)} %get-tuple-element.119), channel_id=1, source_target_pairs={{0,1},{1,2},{2,3},{3,4},{4,5},{5,6},{6,7},{7,8},{8,9},{9,10},{10,1... | collective-permute-start | bytes 16928 | tf_op jit(solution)/shard_map/ppermute | solution.py:22
  65.3 8.0 %collective-permute-start.11 = (f32[94,15]{1,0:T(8,128)S(1)}, f32[94,15]{1,0:T(8,128)S(1)}, u32[]{:S(2)}, u32[]{:S(2)}) collective-permute-start(f32[94,15]{1,0:T(8,128)S(1)} %get-tuple-element.120), channel_id=1, source_target_pairs={{1,0},{2,1},{3,2},{4,3},{5,4},{6,5},{7,6},{8,7},{9,8},{10,9},{11,1... | collective-permute-start | bytes 16928 | tf_op jit(solution)/shard_map/ppermute | solution.py:23
  82.6 5.2 %collective-permute-start.13 = (f32[15,256]{1,0:T(8,128)S(1)}, f32[15,256]{1,0:T(8,128)S(1)}, u32[]{:S(2)}, u32[]{:S(2)}) collective-permute-start(f32[15,256]{1,0:T(8,128)S(1)} %bitcast.706), channel_id=1, source_target_pairs={{16,0},{32,16},{48,32},{64,48},{80,64},{96,80},{112,96},{17,1},{33... | collective-permute-start | bytes 46088 | tf_op jit(solution)/shard_map/ppermute | solution.py:23
  83.9 4.7 %collective-permute-start.12 = (f32[15,256]{1,0:T(8,128)S(1)}, f32[15,256]{1,0:T(8,128)S(1)}, u32[]{:S(2)}, u32[]{:S(2)}) collective-permute-start(f32[15,256]{1,0:T(8,128)S(1)} %bitcast.702), channel_id=1, source_target_pairs={{0,16},{16,32},{32,48},{48,64},{64,80},{80,96},{96,112},{1,17},{17... | collective-permute-start | bytes 46088 | tf_op jit(solution)/shard_map/ppermute | solution.py:22
  89.3 9.3 %collective-permute-start.15 = (f32[94,15]{1,0:T(8,128)}, f32[94,15]{1,0:T(8,128)}, u32[]{:S(2)}, u32[]{:S(2)}) collective-permute-start(f32[94,15]{1,0:T(8,128)} %get-tuple-element.115), channel_id=1, source_target_pairs={{1,0},{2,1},{3,2},{4,3},{5,4},{6,5},{7,6},{8,7},{9,8},{10,9},{11,1... | collective-permute-start | bytes 16928 | tf_op jit(solution)/shard_map/ppermute | solution.py:23
  91.3 8.4 %collective-permute-start.14 = (f32[94,15]{1,0:T(8,128)}, f32[94,15]{1,0:T(8,128)}, u32[]{:S(2)}, u32[]{:S(2)}) collective-permute-start(f32[94,15]{1,0:T(8,128)} %get-tuple-element.116), channel_id=1, source_target_pairs={{0,1},{1,2},{2,3},{3,4},{4,5},{5,6},{6,7},{7,8},{8,9},{9,10},{10,1... | collective-permute-start | bytes 16928 | tf_op jit(solution)/shard_map/ppermute | solution.py:22
  117.8 87.3 %copy-start.47 = (f32[64,256]{1,0:T(8,128)}, f32[64,256]{1,0:T(8,128)S(1)}, u32[]{:S(2)}) copy-start(f32[64,256]{1,0:T(8,128)S(1)} %get-tuple-element.34) | copy-start | bytes 196612
  181.9 2.6 collective-permute-start.16
  183.2 3.1 collective-permute-start.17
  186.4 6.2 %collective-permute-start.18 = (f32[94,15]{1,0:T(8,128)S(1)}, f32[94,15]{1,0:T(8,128)S(1)}, u32[]{:S(2)}, u32[]{:S(2)}) collective-permute-start(f32[94,15]{1,0:T(8,128)S(1)} %get-tuple-element.111), channel_id=1, source_target_pairs={{0,1},{1,2},{2,3},{3,4},{4,5},{5,6},{6,7},{7,8},{8,9},{9,10},{10,1... | collective-permute-start | bytes 16928 | tf_op jit(solution)/shard_map/ppermute | solution.py:22
  188.3 6.1 %collective-permute-start.19 = (f32[94,15]{1,0:T(8,128)S(1)}, f32[94,15]{1,0:T(8,128)S(1)}, u32[]{:S(2)}, u32[]{:S(2)}) collective-permute-start(f32[94,15]{1,0:T(8,128)S(1)} %get-tuple-element.112), channel_id=1, source_target_pairs={{1,0},{2,1},{3,2},{4,3},{5,4},{6,5},{7,6},{8,7},{9,8},{10,9},{11,1... | collective-permute-start | bytes 16928 | tf_op jit(solution)/shard_map/ppermute | solution.py:23
  211.3 4.5 %collective-permute-start.21 = (f32[15,256]{1,0:T(8,128)S(1)}, f32[15,256]{1,0:T(8,128)S(1)}, u32[]{:S(2)}, u32[]{:S(2)}) collective-permute-start(f32[15,256]{1,0:T(8,128)S(1)} %bitcast.707), channel_id=1, source_target_pairs={{16,0},{32,16},{48,32},{64,48},{80,64},{96,80},{112,96},{17,1},{33... | collective-permute-start | bytes 46088 | tf_op jit(solution)/shard_map/ppermute | solution.py:23
  212.6 4.0 collective-permute-start.20
  216.7 6.1 %collective-permute-start.23 = (f32[94,15]{1,0:T(8,128)S(1)}, f32[94,15]{1,0:T(8,128)S(1)}, u32[]{:S(2)}, u32[]{:S(2)}) collective-permute-start(f32[94,15]{1,0:T(8,128)S(1)} %get-tuple-element.107), channel_id=1, source_target_pairs={{1,0},{2,1},{3,2},{4,3},{5,4},{6,5},{7,6},{8,7},{9,8},{10,9},{11,1... | collective-permute-start | bytes 16928 | tf_op jit(solution)/shard_map/ppermute | solution.py:23
  220.4 6.1 %collective-permute-start.22 = (f32[94,15]{1,0:T(8,128)S(1)}, f32[94,15]{1,0:T(8,128)S(1)}, u32[]{:S(2)}, u32[]{:S(2)}) collective-permute-start(f32[94,15]{1,0:T(8,128)S(1)} %get-tuple-element.108), channel_id=1, source_target_pairs={{0,1},{1,2},{2,3},{3,4},{4,5},{5,6},{6,7},{7,8},{8,9},{9,10},{10,1... | collective-permute-start | bytes 16928 | tf_op jit(solution)/shard_map/ppermute | solution.py:22
  293.7 2.6 collective-permute-start.24
  295.0 3.7 collective-permute-start.25
  298.8 6.2 %collective-permute-start.26 = (f32[94,15]{1,0:T(8,128)S(1)}, f32[94,15]{1,0:T(8,128)S(1)}, u32[]{:S(2)}, u32[]{:S(2)}) collective-permute-start(f32[94,15]{1,0:T(8,128)S(1)} %get-tuple-element.103), channel_id=1, source_target_pairs={{0,1},{1,2},{2,3},{3,4},{4,5},{5,6},{6,7},{7,8},{8,9},{9,10},{10,1... | collective-permute-start | bytes 16928 | tf_op jit(solution)/shard_map/ppermute | solution.py:22
  300.8 6.1 %collective-permute-start.27 = (f32[94,15]{1,0:T(8,128)S(1)}, f32[94,15]{1,0:T(8,128)S(1)}, u32[]{:S(2)}, u32[]{:S(2)}) collective-permute-start(f32[94,15]{1,0:T(8,128)S(1)} %get-tuple-element.104), channel_id=1, source_target_pairs={{1,0},{2,1},{3,2},{4,3},{5,4},{6,5},{7,6},{8,7},{9,8},{10,9},{11,1... | collective-permute-start | bytes 16928 | tf_op jit(solution)/shard_map/ppermute | solution.py:23
  323.7 5.2 %collective-permute-start.29 = (f32[15,256]{1,0:T(8,128)S(1)}, f32[15,256]{1,0:T(8,128)S(1)}, u32[]{:S(2)}, u32[]{:S(2)}) collective-permute-start(f32[15,256]{1,0:T(8,128)S(1)} %bitcast.708), channel_id=1, source_target_pairs={{16,0},{32,16},{48,32},{64,48},{80,64},{96,80},{112,96},{17,1},{33... | collective-permute-start | bytes 46088 | tf_op jit(solution)/shard_map/ppermute | solution.py:23
  325.0 4.7 %collective-permute-start.28 = (f32[15,256]{1,0:T(8,128)S(1)}, f32[15,256]{1,0:T(8,128)S(1)}, u32[]{:S(2)}, u32[]{:S(2)}) collective-permute-start(f32[15,256]{1,0:T(8,128)S(1)} %bitcast.704), channel_id=1, source_target_pairs={{0,16},{16,32},{32,48},{48,64},{64,80},{80,96},{96,112},{1,17},{17... | collective-permute-start | bytes 46088 | tf_op jit(solution)/shard_map/ppermute | solution.py:22
  329.7 6.1 %collective-permute-start.31 = (f32[94,15]{1,0:T(8,128)S(1)}, f32[94,15]{1,0:T(8,128)S(1)}, u32[]{:S(2)}, u32[]{:S(2)}) collective-permute-start(f32[94,15]{1,0:T(8,128)S(1)} %get-tuple-element.99), channel_id=1, source_target_pairs={{1,0},{2,1},{3,2},{4,3},{5,4},{6,5},{7,6},{8,7},{9,8},{10,9},{11,1... | collective-permute-start | bytes 16928 | tf_op jit(solution)/shard_map/ppermute | solution.py:23
  333.4 6.0 %collective-permute-start.30 = (f32[94,15]{1,0:T(8,128)S(1)}, f32[94,15]{1,0:T(8,128)S(1)}, u32[]{:S(2)}, u32[]{:S(2)}) collective-permute-start(f32[94,15]{1,0:T(8,128)S(1)} %get-tuple-element.100), channel_id=1, source_target_pairs={{0,1},{1,2},{2,3},{3,4},{4,5},{5,6},{6,7},{7,8},{8,9},{9,10},{10,1... | collective-permute-start | bytes 16928 | tf_op jit(solution)/shard_map/ppermute | solution.py:22
  344.7 60.8 %copy-start.46 = (f32[64,256]{1,0:T(8,128)S(1)}, f32[64,256]{1,0:T(8,128)}, u32[]{:S(2)}) copy-start(f32[64,256]{1,0:T(8,128)} %param.4) | copy-start | bytes 196612
  344.7 60.8 %copy-start.48 = (f32[64,256]{1,0:T(8,128)S(1)}, f32[64,256]{1,0:T(8,128)}, u32[]{:S(2)}) copy-start(f32[64,256]{1,0:T(8,128)} %copy-done.47) | copy-start | bytes 196612
  344.8 60.8 %copy-start.49 = (f32[64,256]{1,0:T(8,128)S(1)}, f32[64,256]{1,0:T(8,128)}, u32[]{:S(2)}) copy-start(f32[64,256]{1,0:T(8,128)} %get-tuple-element.33) | copy-start | bytes 196612
  (44 other events, 687.9 us)
